TPU v7x, 32 devices: a whole 2x2x4 slice. The times are simulated.
32 devices in a mesh: tm: 4 (over y, x), rows: 2 (over core), batch: 4 (over z).
Axes of the slice: x: 2, y: 2, z: 4, core: 2. Of those that a mesh axis runs over, the one named last changes fastest.
Arguments:
- inputs: bfloat16 [4, 8, 16, 128, 384], P('batch', 'tm', 'rows'), parts along dimension 0, may hold values from -16 to 16
- norm_gain: float32 [384], replicated, may hold values from 0.1 to 1.9
- norm_bias: float32 [384], replicated, may hold values from -3 to 3
- conv_weight: bfloat16 [3, 3, 3, 384, 384], replicated, may hold values from -0.0625 to 0.0625
- conv_bias: float32 [384], replicated, may hold values from -2 to 2
Outputs:
- decoded: bfloat16 [4, 8, 16, 128, 384], P('batch', 'tm', 'rows'), parts along dimension 0
There are 4 independent parts, one for each index of `batch`. A program takes and returns all parts, laid end to end along the dimension named above; an argument that names none is the same for every part. Nothing has to cross between parts.
All inputs are finite; a program needn't handle non-finite values.
Results may differ from a plain program's by a relative error of at most 0.0025.
Values may be sent and summed in bfloat16 or wider, within the bound.
A program may use at most 128 MiB of HBM per device.

v0:
```python
import jax
import jax.numpy as jnp
from jax import lax
from jax.sharding import PartitionSpec as P

GROUPS = 32


epsilon = 1e-06


def from_behind(value, axis, steps):
    count = lax.axis_size(axis)
    initial, last = (max(0, -steps), min(count, count - steps))
    return lax.ppermute(value, axis, [(source, source + steps) for source in range(initial, last)])


def with_halo(block, sides, width):
    for axis, dim in sides:
        count = lax.axis_size(axis)
        forward = [(i, i + 1) for i in range(count - 1)]
        backward = [(target, source) for source, target in forward]
        low = lax.ppermute(
            lax.slice_in_dim(block, block.shape[dim] - width, None, axis=dim), axis, forward
        )
        high = lax.ppermute(lax.slice_in_dim(block, 0, width, axis=dim), axis, backward)
        block = jnp.concatenate([low, block, high], axis=dim)
    return block


def convolve(padded, conv_weight, frames, height, width_dev):
    channels = padded.shape[-1]
    summed = jnp.zeros(
        (padded.shape[0] * frames * height * width_dev, conv_weight.shape[-1]), jnp.float32
    )
    for tap_time in range(3):
        for tap_row in range(3):
            slab_rows = padded[:, tap_time : tap_time + frames, tap_row : tap_row + height]
            columns = jnp.concatenate(
                [
                    slab_rows[:, :, :, 0:width_dev],
                    slab_rows[:, :, :, 1 : width_dev + 1],
                    slab_rows[:, :, :, 2 : width_dev + 2],
                ],
                axis=-1,
            )
            kernel = conv_weight[tap_time, tap_row].reshape(3 * channels, -1)
            summed = summed + jnp.dot(
                columns.reshape(-1, 3 * channels), kernel, preferred_element_type=jnp.float32
            )
    return summed


def grouped(chan_values, per_group):
    return jnp.sum(chan_values.reshape(-1, per_group), axis=1)


def shards(inputs, norm_gain, norm_bias, conv_weight, conv_bias):
    values = inputs.astype(jnp.float32)
    clip_count, frames, height, width_dev, channels = inputs.shape
    per_group = channels // GROUPS
    cell_count = (
        1.0
        * clip_count
        * frames
        * height
        * width_dev
        * per_group
        * lax.axis_size("tm")
        * lax.axis_size("rows")
    )
    chan_sum = jnp.sum(values, axis=(0, 1, 2, 3))
    chan_raw = jnp.sum(values * values, axis=(0, 1, 2, 3))
    total_sum, total_square = lax.psum(
        (grouped(chan_sum, per_group), grouped(chan_raw, per_group)), ("tm", "rows")
    )
    group_mean = total_sum / cell_count
    group_var = total_square / cell_count - group_mean * group_mean
    centered = values - jnp.repeat(group_mean, per_group)
    inverse = jnp.repeat(lax.rsqrt(group_var + epsilon), per_group)
    normed = centered * inverse * norm_gain + norm_bias
    active = (normed * jax.nn.sigmoid(normed)).astype(jnp.bfloat16)
    earlier = from_behind(active, "tm", 1)
    extended = with_halo(jnp.concatenate([earlier, active], axis=1), (("rows", 2),), 1)
    padded = jnp.pad(extended, ((0, 0), (0, 0), (0, 0), (1, 1), (0, 0)))
    summed = convolve(padded, conv_weight, frames, height, width_dev)
    result = values + summed.reshape(values.shape) + conv_bias
    return result.astype(jnp.bfloat16)


def solution(mesh):
    placed = (P("batch", "tm", "rows", None, None), P(), P(), P(), P())
    return jax.shard_map(
        shards,
        mesh=mesh,
        in_specs=placed,
        out_specs=P("batch", "tm", "rows", None, None),
        check_vma=False,
    )
```

profile of v0, /device:TPU:20, one launch (start us, length us, event | category | flops | bytes accessed | tf_op | source)
XLA Modules:
  0.0 137.7 jit_solution(7587805098458186710)
XLA Ops:
  0.0 1.9 %convert_reduce_fusion = (f32[384]{0:T(512)S(1)}, f32[384]{0:T(512)S(1)}) fusion(bf16[1,2,8,128,384]{4,3,2,1,0:T(8,128)(2,1)} %param.5), kind=kLoop, calls=%fused_computation.6 | loop fusion | flops 3144960 | bytes 1575936 | tf_op jit(solution)/shard_map/reduce_sum | solution.py:72
  2.3 12.7 %all-reduce.1 = (f32[32]{0:T(128)S(1)}, f32[32]{0:T(128)S(1)}) all-reduce(f32[32]{0:T(128)S(1)} %reduce_sum.39, f32[32]{0:T(128)S(1)} %reduce_sum.37), channel_id=1, replica_groups=mesh['tm'=4,'rows'=2,'batch'=4] {'tm','rows'}, use_global_device_ids=true, to_apply=%region_5.0 | all-reduce | flops 64 | bytes 512 | tf_op jit(solution)/shard_map/psum | solution.py:74
  15.4 2.5 %fusion.14 = bf16[1,2,8,128,384]{4,3,2,1,0:T(8,128)(2,1)S(1)} fusion(bf16[1,2,8,128,384]{4,3,2,1,0:T(8,128)(2,1)} %param.5, f32[384]{0:T(512)} %param.7, f32[384]{0:T(512)} %param.6, f32[384]{0:T(512)S(1)} %mul.29, f32[384]{0:T(512)S(1)} %sub.13), kind=kLoop, calls=%fused_computation.33 | loop fusion | flops 7864320 | bytes 3151872 | tf_op jit(solution)/shard_map/convert_element_type | solution.py:82
  17.9 1.9 %collective-permute-start = (bf16[1,2,8,128,384]{4,3,2,1,0:T(8,128)(2,1)S(1)}, bf16[1,2,8,128,384]{4,3,2,1,0:T(8,128)(2,1)S(1)}, u32[]{:S(2)}, u32[]{:S(2)}) collective-permute-start(bf16[1,2,8,128,384]{4,3,2,1,0:T(8,128)(2,1)S(1)} %fusion.14), channel_id=1, source_target_pairs={{0,8},{8,16},{16,24},{1,9},{9,17},{17,25},{2,10},{10,18},{18,26},{... | collective-permute-start | bytes 4718600 | tf_op jit(solution)/shard_map/ppermute | solution.py:15
  19.8 36.2 %collective-permute-done = bf16[1,2,8,128,384]{4,3,2,1,0:T(8,128)(2,1)S(1)} collective-permute-done((bf16[1,2,8,128,384]{4,3,2,1,0:T(8,128)(2,1)S(1)}, bf16[1,2,8,128,384]{4,3,2,1,0:T(8,128)(2,1)S(1)}, u32[]{:S(2)}, u32[]{:S(2)}) %collective-permute-start) | collective-permute-done | bytes 1572896 | tf_op jit(solution)/shard_map/ppermute | solution.py:15
  56.1 1.3 collective-permute-start.1
  57.4 1.5 %collective-permute-start.2 = (bf16[1,4,1,128,384]{4,3,2,1,0:T(8,128)(2,1)S(1)}, bf16[1,4,1,128,384]{4,3,2,1,0:T(8,128)(2,1)S(1)}, u32[]{:S(2)}, u32[]{:S(2)}) collective-permute-start(bf16[1,4,1,128,384]{4,3,2,1,0:T(8,128)(2,1)S(1)} %get-tuple-element.45), channel_id=1, source_target_pairs={{4,0},{5,1},{6,2},{7,3},{12,8},{13,9},{14,10},{15,11},{20,16},{21,... | collective-permute-start | bytes 1179656 | tf_op jit(solution)/shard_map/ppermute | solution.py:26
  58.9 5.8 %fusion.18 = (bf16[1,1,3,384,384]{4,3,2,1,0:T(8,128)(2,1)}, bf16[1,1,3,384,384]{4,3,2,1,0:T(8,128)(2,1)}, bf16[1,1,3,384,384]{4,3,2,1,0:T(8,128)(2,1)}, bf16[1,1...) fusion(bf16[3,3,3,384,384]{4,3,2,1,0:T(8,128)(2,1)} %param.8), kind=kLoop, calls=%fused_computation.42 | loop fusion | bytes 15925248 | tf_op jit(solution)/shard_map/slice | solution.py:47
  64.7 1.9 %select_maximum_fusion = bf16[1,4,10,130,384]{4,3,2,1,0:T(8,128)(2,1)S(1)} fusion(bf16[1,4,1,128,384]{4,3,2,1,0:T(8,128)(2,1)S(1)} %collective-permute-done.2, bf16[1,4,1,128,384]{4,3,2,1,0:T(8,128)(2,1)S(1)} %collective-permute-done.1, bf16[1,2,8,128,384]{4,3,2,1,0:T(8,128)(2,1)S(1)} %fusion.14, bf16[1,2,8,128,384]{4,3,2,1,0:T(8,128)(2,1)S(1)} %collective-permute-done), kind=kLoop, calls=%fused_computation.18 | loop fusion | flops 29952000 | bytes 7925760 | tf_op jit(solution)/shard_map/concatenate | solution.py:27
  66.6 10.3 %fusion.19 = (bf16[1,2,8,128,384]{4,3,2,1,0:T(8,128)(2,1)S(1)}, bf16[1,2,8,128,384]{4,3,2,1,0:T(8,128)(2,1)S(1)}, bf16[1,2,8,128,384]{4,3,2,1,0:T(8,128)(2,1)S(1...) fusion(bf16[1,4,10,130,384]{4,3,2,1,0:T(8,128)(2,1)S(1)} %selec, ...), kind=kLoop, calls=%fused_computation.43 | loop fusion | bytes 56623104 | tf_op jit(solution)/shard_map/slice | solution.py:41
  76.8 1.1 pad_maximum_fusion.9
  78.0 1.1 fusion.20
  79.8 0.7 pad_maximum_fusion.1
  81.0 4.5 %fusion.22 = f32[2048,384]{1,0:T(8,128)} fusion(bf16[2048,1152]{1,0:T(8,128)(2,1)S(1)} %bitcast.42, bf16[1152,384]{1,0:T(8,128)(2,1)S(1)} %bitcast.55), kind=kOutput, calls=%fused_computation.46 | convolution fusion | flops 1811939328 | bytes 8749056 | tf_op jit(solution)/shard_map/dot_general | solution.py:48
  85.5 0.7 pad_maximum_fusion.3
  86.6 4.6 %fusion.24 = f32[2048,384]{1,0:T(8,128)} fusion(bf16[2048,1152]{1,0:T(8,128)(2,1)S(1)} %bitcast.43, bf16[1152,384]{1,0:T(8,128)(2,1)S(1)} %bitcast.54), kind=kOutput, calls=%fused_computation.48 | convolution fusion | flops 1811939328 | bytes 8749056 | tf_op jit(solution)/shard_map/dot_general | solution.py:48
  91.3 0.9 pad_maximum_fusion.4
  92.4 4.5 %fusion.25 = f32[2048,384]{1,0:T(8,128)} fusion(bf16[2048,1152]{1,0:T(8,128)(2,1)S(1)} %bitcast.44, bf16[1152,384]{1,0:T(8,128)(2,1)S(1)} %bitcast.53), kind=kOutput, calls=%fused_computation.49 | convolution fusion | flops 1811939328 | bytes 8749056 | tf_op jit(solution)/shard_map/dot_general | solution.py:48
  96.9 0.7 pad_maximum_fusion.5
  98.1 4.6 %fusion.27 = f32[2048,384]{1,0:T(8,128)} fusion(bf16[2048,1152]{1,0:T(8,128)(2,1)S(1)} %bitcast.45, bf16[1152,384]{1,0:T(8,128)(2,1)S(1)} %bitcast.52), kind=kOutput, calls=%fused_computation.51 | convolution fusion | flops 1811939328 | bytes 8749056 | tf_op jit(solution)/shard_map/dot_general | solution.py:48
  102.7 0.7 pad_maximum_fusion.6
  103.8 4.5 %fusion.28 = f32[2048,384]{1,0:T(8,128)} fusion(bf16[2048,1152]{1,0:T(8,128)(2,1)S(1)} %bitcast.46, bf16[1152,384]{1,0:T(8,128)(2,1)S(1)} %bitcast.51), kind=kOutput, calls=%fused_computation.52 | convolution fusion | flops 1811939328 | bytes 8749056 | tf_op jit(solution)/shard_map/dot_general | solution.py:48
  108.3 3.2 %pad_maximum_fusion.2 = (bf16[1,2,8,128,1152]{4,3,2,1,0:T(8,128)(2,1)S(1)}, bf16[1,2,8,128,1152]{4,3,2,1,0:T(8,128)(2,1)}, bf16[1,2,8,128,1152]{4,3,2,1,0:T(8,128)(2,1)S(1)}) fusion(bf16[1,2,8,128,384]{4,3,2,1,0:T(8,128)(2,1)S(1)} %copy-done.1, bf16[1,2,8,128,384]{4,3,2,1,0:T(8,128)(2,1)S(1)} %collective-permute-done, ...), kind=kLoop, calls=%fused_computation.11 | loop fusion | flops 47185920 | bytes 26738688 | tf_op jit(solution)/shard_map/concatenate | solution.py:39
  111.6 4.5 %fusion.23 = f32[2048,384]{1,0:T(8,128)} fusion(bf16[2048,1152]{1,0:T(8,128)(2,1)S(1)} %bitcast.41, bf16[1152,384]{1,0:T(8,128)(2,1)S(1)} %bitcast.50), kind=kOutput, calls=%fused_computation.47 | convolution fusion | flops 1811939328 | bytes 8749056 | tf_op jit(solution)/shard_map/dot_general | solution.py:48
  116.1 4.5 %fusion.26 = f32[2048,384]{1,0:T(8,128)} fusion(bf16[2048,1152]{1,0:T(8,128)(2,1)S(1)} %bitcast.40, bf16[1152,384]{1,0:T(8,128)(2,1)S(1)} %bitcast.49), kind=kOutput, calls=%fused_computation.50 | convolution fusion | flops 1811939328 | bytes 8749056 | tf_op jit(solution)/shard_map/dot_general | solution.py:48
  120.6 4.5 %fusion.29 = f32[2048,384]{1,0:T(8,128)} fusion(bf16[2048,1152]{1,0:T(8,128)(2,1)S(1)} %bitcast.39, bf16[1152,384]{1,0:T(8,128)(2,1)S(1)} %bitcast.48), kind=kOutput, calls=%fused_computation.53 | convolution fusion | flops 1811939328 | bytes 8749056 | tf_op jit(solution)/shard_map/dot_general | solution.py:48
  125.1 0.7 pad_maximum_fusion.8
  125.8 0.5 copy-done.14
  126.3 1.0 copy-done.15
  127.3 1.0 copy-done.16
  128.2 7.7 %add_add_fusion = f32[2048,384]{1,0:T(8,128)S(1)} fusion(f32[2048,384]{1,0:T(8,128)} %fusion.29, f32[2048,384]{1,0:T(8,128)} %fusion.28, f32[2048,384]{1,0:T(8,128)} %fusion.27, f32[2048,384]{1,0:T(8,128)} %fusion.26, f32[2048,384]{1,0:T(8,128)S(1)} %copy-done.17, f32[2048,384]{1,0:T(8,128)S(1)} %copy-done.16, f32[2048,384]{1,0:T(8,128)S(1)} %copy-done.15, ...), kind=kOutput, calls=%fused_computation.37 | convolution fusion | flops 1818230784 | bytes 33914880 | tf_op jit(solution)/shard_map/dot_general | solution.py:48
  136.0 1.7 %fusion.17 = bf16[1,2,8,128,384]{4,3,2,1,0:T(8,128)(2,1)} fusion(f32[1,2,8,128,384]{4,3,2,1,0:T(8,128)S(1)} %bitcast.38, bf16[1,2,8,128,384]{4,3,2,1,0:T(8,128)(2,1)S(1)} %copy-done, f32[384]{0:T(512)S(1)} %copy-done.26), kind=kLoop, calls=%fused_computation.36 | loop fusion | flops 3145728 | bytes 6292992 | tf_op jit(solution)/shard_map/convert_element_type | solution.py:88
  (63 shorter events, 3.8 us)
Async XLA Ops:
  17.9 38.1 %collective-permute-start = (bf16[1,2,8,128,384]{4,3,2,1,0:T(8,128)(2,1)S(1)}, bf16[1,2,8,128,384]{4,3,2,1,0:T(8,128)(2,1)S(1)}, u32[]{:S(2)}, u32[]{:S(2)}) collective-permute-start(bf16[1,2,8,128,384]{4,3,2,1,0:T(8,128)(2,1)S(1)} %fusion.14), channel_id=1, source_target_pairs={{0,8},{8,16},{16,24},{1,9},{9,17},{17,25},{2,10},{10,18},{18,26},{... | collective-permute-start | bytes 4718600 | tf_op jit(solution)/shard_map/ppermute | solution.py:15
  56.1 8.6 %collective-permute-start.1 = (bf16[1,4,1,128,384]{4,3,2,1,0:T(8,128)(2,1)S(1)}, bf16[1,4,1,128,384]{4,3,2,1,0:T(8,128)(2,1)S(1)}, u32[]{:S(2)}, u32[]{:S(2)}) collective-permute-start(bf16[1,4,1,128,384]{4,3,2,1,0:T(8,128)(2,1)S(1)} %get-tuple-element.44), channel_id=1, source_target_pairs={{0,4},{1,5},{2,6},{3,7},{8,12},{9,13},{10,14},{11,15},{16,20},{17,... | collective-permute-start | bytes 1179656 | tf_op jit(solution)/shard_map/ppermute | solution.py:23
  57.4 7.3 %collective-permute-start.2 = (bf16[1,4,1,128,384]{4,3,2,1,0:T(8,128)(2,1)S(1)}, bf16[1,4,1,128,384]{4,3,2,1,0:T(8,128)(2,1)S(1)}, u32[]{:S(2)}, u32[]{:S(2)}) collective-permute-start(bf16[1,4,1,128,384]{4,3,2,1,0:T(8,128)(2,1)S(1)} %get-tuple-element.45), channel_id=1, source_target_pairs={{4,0},{5,1},{6,2},{7,3},{12,8},{13,9},{14,10},{15,11},{20,16},{21,... | collective-permute-start | bytes 1179656 | tf_op jit(solution)/shard_map/ppermute | solution.py:26
  77.9 1.4 %copy-start.11 = (bf16[1,2,8,128,384]{4,3,2,1,0:T(8,128)(2,1)S(1)}, bf16[1,2,8,128,384]{4,3,2,1,0:T(8,128)(2,1)}, u32[]{:S(2)}) copy-start(bf16[1,2,8,128,384]{4,3,2,1,0:T(8,128)(2,1)} %get-tuple-element.33) | copy-start | bytes 4718596
  77.9 1.9 %copy-start.12 = (bf16[1,2,8,128,384]{4,3,2,1,0:T(8,128)(2,1)S(1)}, bf16[1,2,8,128,384]{4,3,2,1,0:T(8,128)(2,1)}, u32[]{:S(2)}) copy-start(bf16[1,2,8,128,384]{4,3,2,1,0:T(8,128)(2,1)} %get-tuple-element.34) | copy-start | bytes 4718596
  79.8 1.2 copy-start.25
  81.0 4.5 %copy-start.9 = (bf16[1,2,8,128,384]{4,3,2,1,0:T(8,128)(2,1)S(1)}, bf16[1,2,8,128,384]{4,3,2,1,0:T(8,128)(2,1)}, u32[]{:S(2)}) copy-start(bf16[1,2,8,128,384]{4,3,2,1,0:T(8,128)(2,1)} %get-tuple-element.29) | copy-start | bytes 4718596
  81.0 4.5 %copy-start.10 = (bf16[1,2,8,128,384]{4,3,2,1,0:T(8,128)(2,1)S(1)}, bf16[1,2,8,128,384]{4,3,2,1,0:T(8,128)(2,1)}, u32[]{:S(2)}) copy-start(bf16[1,2,8,128,384]{4,3,2,1,0:T(8,128)(2,1)} %get-tuple-element.30) | copy-start | bytes 4718596
  85.5 1.2 copy-start.24
  86.6 4.6 %copy-start.7 = (bf16[1,2,8,128,384]{4,3,2,1,0:T(8,128)(2,1)S(1)}, bf16[1,2,8,128,384]{4,3,2,1,0:T(8,128)(2,1)}, u32[]{:S(2)}) copy-start(bf16[1,2,8,128,384]{4,3,2,1,0:T(8,128)(2,1)} %get-tuple-element.27) | copy-start | bytes 4718596
  86.6 4.6 %copy-start.8 = (bf16[1,2,8,128,384]{4,3,2,1,0:T(8,128)(2,1)S(1)}, bf16[1,2,8,128,384]{4,3,2,1,0:T(8,128)(2,1)}, u32[]{:S(2)}) copy-start(bf16[1,2,8,128,384]{4,3,2,1,0:T(8,128)(2,1)} %get-tuple-element.28) | copy-start | bytes 4718596
  91.3 1.2 copy-start.23
  92.4 4.5 %copy-start.5 = (bf16[1,2,8,128,384]{4,3,2,1,0:T(8,128)(2,1)S(1)}, bf16[1,2,8,128,384]{4,3,2,1,0:T(8,128)(2,1)}, u32[]{:S(2)}) copy-start(bf16[1,2,8,128,384]{4,3,2,1,0:T(8,128)(2,1)} %get-tuple-element.23) | copy-start | bytes 4718596
  92.4 4.5 %copy-start.6 = (bf16[1,2,8,128,384]{4,3,2,1,0:T(8,128)(2,1)S(1)}, bf16[1,2,8,128,384]{4,3,2,1,0:T(8,128)(2,1)}, u32[]{:S(2)}) copy-start(bf16[1,2,8,128,384]{4,3,2,1,0:T(8,128)(2,1)} %get-tuple-element.24) | copy-start | bytes 4718596
  96.9 1.2 copy-start.22
  98.1 4.6 %copy-start.3 = (bf16[1,2,8,128,384]{4,3,2,1,0:T(8,128)(2,1)S(1)}, bf16[1,2,8,128,384]{4,3,2,1,0:T(8,128)(2,1)}, u32[]{:S(2)}) copy-start(bf16[1,2,8,128,384]{4,3,2,1,0:T(8,128)(2,1)} %get-tuple-element.21) | copy-start | bytes 4718596
  98.1 4.6 %copy-start.4 = (bf16[1,2,8,128,384]{4,3,2,1,0:T(8,128)(2,1)S(1)}, bf16[1,2,8,128,384]{4,3,2,1,0:T(8,128)(2,1)}, u32[]{:S(2)}) copy-start(bf16[1,2,8,128,384]{4,3,2,1,0:T(8,128)(2,1)} %get-tuple-element.22) | copy-start | bytes 4718596
  102.7 1.2 copy-start.21
  103.8 4.5 %copy-start.1 = (bf16[1,2,8,128,384]{4,3,2,1,0:T(8,128)(2,1)S(1)}, bf16[1,2,8,128,384]{4,3,2,1,0:T(8,128)(2,1)}, u32[]{:S(2)}) copy-start(bf16[1,2,8,128,384]{4,3,2,1,0:T(8,128)(2,1)} %get-tuple-element.31) | copy-start | bytes 4718596
  103.8 4.5 %copy-start.2 = (bf16[1,2,8,128,384]{4,3,2,1,0:T(8,128)(2,1)S(1)}, bf16[1,2,8,128,384]{4,3,2,1,0:T(8,128)(2,1)}, u32[]{:S(2)}) copy-start(bf16[1,2,8,128,384]{4,3,2,1,0:T(8,128)(2,1)} %get-tuple-element.32) | copy-start | bytes 4718596
  108.3 3.2 %copy-start.20 = (bf16[1,1,3,384,384]{4,3,2,1,0:T(8,128)(2,1)S(1)}, bf16[1,1,3,384,384]{4,3,2,1,0:T(8,128)(2,1)}, u32[]{:S(2)}) copy-start(bf16[1,1,3,384,384]{4,3,2,1,0:T(8,128)(2,1)} %get-tuple-element.15) | copy-start | bytes 2654212
  111.6 4.5 %copy-start.13 = (bf16[1,2,8,128,1152]{4,3,2,1,0:T(8,128)(2,1)S(1)}, bf16[1,2,8,128,1152]{4,3,2,1,0:T(8,128)(2,1)}, u32[]{:S(2)}) copy-start(bf16[1,2,8,128,1152]{4,3,2,1,0:T(8,128)(2,1)} %get-tuple-element.47) | copy-start | bytes 14155780
  111.6 4.5 %copy-start.19 = (bf16[1,1,3,384,384]{4,3,2,1,0:T(8,128)(2,1)S(1)}, bf16[1,1,3,384,384]{4,3,2,1,0:T(8,128)(2,1)}, u32[]{:S(2)}) copy-start(bf16[1,1,3,384,384]{4,3,2,1,0:T(8,128)(2,1)} %get-tuple-element.12) | copy-start | bytes 2654212
  116.1 4.5 %copy-start.18 = (bf16[1,1,3,384,384]{4,3,2,1,0:T(8,128)(2,1)S(1)}, bf16[1,1,3,384,384]{4,3,2,1,0:T(8,128)(2,1)}, u32[]{:S(2)}) copy-start(bf16[1,1,3,384,384]{4,3,2,1,0:T(8,128)(2,1)} %get-tuple-element.17) | copy-start | bytes 2654212
  120.5 5.2 %copy-start.17 = (f32[2048,384]{1,0:T(8,128)S(1)}, f32[2048,384]{1,0:T(8,128)}, u32[]{:S(2)}) copy-start(f32[2048,384]{1,0:T(8,128)} %fusion.25) | copy-start | bytes 9437188
  125.1 1.2 copy-start.14
  125.1 2.2 %copy-start.15 = (f32[2048,384]{1,0:T(8,128)S(1)}, f32[2048,384]{1,0:T(8,128)}, u32[]{:S(2)}) copy-start(f32[2048,384]{1,0:T(8,128)} %fusion.22) | copy-start | bytes 9437188
  125.1 3.1 %copy-start.16 = (f32[2048,384]{1,0:T(8,128)S(1)}, f32[2048,384]{1,0:T(8,128)}, u32[]{:S(2)}) copy-start(f32[2048,384]{1,0:T(8,128)} %fusion.24) | copy-start | bytes 9437188
  128.2 7.7 %copy-start = (bf16[1,2,8,128,384]{4,3,2,1,0:T(8,128)(2,1)S(1)}, bf16[1,2,8,128,384]{4,3,2,1,0:T(8,128)(2,1)}, u32[]{:S(2)}) copy-start(bf16[1,2,8,128,384]{4,3,2,1,0:T(8,128)(2,1)} %param.5) | copy-start | bytes 4718596
  128.2 7.7 %copy-start.26 = (f32[384]{0:T(512)S(1)}, f32[384]{0:T(512)}, u32[]{:S(2)}) copy-start(f32[384]{0:T(512)} %param.9) | copy-start | bytes 4612
where the time goes:
time: 139 us; the launch traced here: 138 us
  matrix products  43.9 us (32%)
  waiting for transfers between devices  36.2 us (26%)
  local copies, waits for them, and re-layouts  23.1 us (17%)
  other arithmetic  17 us (12%)
  blocking collectives  12.7 us (9%)
  starting transfers between devices  4.71 us (3%)
    dot_general x9, matrix products, convolve(): jnp.dot(columns.reshape(-1, 3 * channels), kernel, preferred_element_type...  43.9 us
    ppermute x1, waiting for transfers between devices, from_behind(): lax.ppermute(value, axis, [(source, source + steps) for source in range(i...  36.2 us
    psum x1, blocking collectives, shards(): lax.psum((grouped(chan_sum, per_group), grouped(chan_raw, per_group)), ('...  12.7 us
    slice x1, local copies, waits for them, and re-layouts, convolve(): slab_rows[:, :, :, 0:width_dev]  10.3 us
    concatenate x7, other arithmetic, convolve(): jnp.concatenate([slab_rows[:, :, :, 0:width_dev], slab_rows[:, :, :, 1:wi...  7.53 us
    slice x1, local copies, waits for them, and re-layouts, convolve(): kernel = conv_weight[tap_time, tap_row].reshape(3 * channels, -1)  5.77 us
    unnamed x54, local copies, waits for them, and re-layouts  5.37 us
    concatenate x2, other arithmetic, with_halo(): block = jnp.concatenate([low, block, high], axis=dim)  2.96 us
  transfers between devices with their start and end apart: 3, of which 1 were waited for; matrix products, arithmetic and copies ran while one was open for 4% of the time, Pallas kernels for 0%

commit v1 on v0

v1 whole, which is shorter than its diff:
```python
import functools

import jax
import jax.numpy as jnp
from jax import lax
from jax.experimental import pallas as pl
from jax.experimental.pallas import tpu as pltpu
from jax.sharding import PartitionSpec as P

GROUPS = 32
MESH = pl.DeviceIdType.MESH
OWN_ROWS = 2

epsilon = 1e-06


def block_kernel(
    T, R, x_hbm, gain_ref, nbias_ref, w_hbm, cbias_ref, out_ref,
    xv, wv, hraw, eown, ehalo, own3, halo3, edge3, acc, stats,
    x_sem, w_sem, halo_send, halo_recv, eown_send, eown_recv,
    ehalo_send, ehalo_recv, stat_send, stat_recv,
):
    F, H, W, C = x_hbm.shape
    C3 = 3 * C
    n = T * R
    tm = lax.axis_index("tm")
    row = lax.axis_index("rows")
    me = tm * R + row

    def peer(offset):
        other = lax.rem(me + offset, n)
        return {"tm": other // R, "rows": lax.rem(other, R)}

    x_copies = [pltpu.make_async_copy(x_hbm.at[f], xv.at[f], x_sem.at[f]) for f in range(F)]
    w_copies = [
        pltpu.make_async_copy(
            w_hbm.at[kt, kh], wv.at[kt, :, pl.ds(kh * C, C)], w_sem.at[kt * 3 + kh]
        )
        for kt in range(3)
        for kh in range(3)
    ]
    barrier = pltpu.get_barrier_semaphore()
    for d in range(1, n):
        pl.semaphore_signal(barrier, inc=1, device_id=peer(d), device_id_type=MESH)
    for c in x_copies:
        c.start()
    pl.semaphore_wait(barrier, n - 1)

    def row_of(i):
        return jnp.where(i == 0, 0, jnp.where(i == 1, H - 1, i - 1))

    def halo_copy(i, r):
        return pltpu.make_async_remote_copy(
            src_ref=x_hbm.at[pl.ds(F - 2, 2), pl.ds(r, 1)],
            dst_ref=hraw.at[:, pl.ds(r, 1)],
            send_sem=halo_send.at[i],
            recv_sem=halo_recv.at[i],
            device_id={"tm": lax.rem(tm + 1, T), "rows": row},
            device_id_type=MESH,
        )

    def own_edge(side):
        r = H - 1 if side == 0 else 0
        target = row + 1 if side == 0 else row - 1
        return pltpu.make_async_remote_copy(
            src_ref=x_hbm.at[:, pl.ds(r, 1)],
            dst_ref=eown.at[side],
            send_sem=eown_send.at[side],
            recv_sem=eown_recv.at[side],
            device_id={"tm": tm, "rows": lax.rem(target + R, R)},
            device_id_type=MESH,
        )

    def halo_edge(side):
        r = H - 1 if side == 0 else 0
        target = row + 1 if side == 0 else row - 1
        return pltpu.make_async_remote_copy(
            src_ref=hraw.at[:, pl.ds(r, 1)],
            dst_ref=ehalo.at[side],
            send_sem=ehalo_send.at[side],
            recv_sem=ehalo_recv.at[side],
            device_id={"tm": tm, "rows": lax.rem(target + R, R)},
            device_id_type=MESH,
        )

    has_next, has_prev = tm < T - 1, tm > 0
    sends_edge = (row < R - 1, row > 0)
    gets_edge = (row > 0, row < R - 1)

    @pl.when(has_next)
    def _():
        for i in range(H):
            halo_copy(i, 0 if i == 0 else H - 1 if i == 1 else i - 1).start()

    for side in range(2):
        @pl.when(sends_edge[side])
        def _():
            own_edge(side).start()

    for c in w_copies:
        c.start()

    total = jnp.zeros((8, C), jnp.float32)
    square = jnp.zeros((8, C), jnp.float32)
    for f in range(F):
        x_copies[f].wait()

        def add_rows(r, carry):
            v = xv[f, r].astype(jnp.float32).reshape(W // 8, 8, C)
            return carry[0] + jnp.sum(v, axis=0), carry[1] + jnp.sum(v * v, axis=0)

        total, square = lax.fori_loop(0, H, add_rows, (total, square))
    stats[0, 0:8] = total
    stats[0, 8:16] = square

    def stat_copy(d):
        return pltpu.make_async_remote_copy(
            src_ref=stats.at[0],
            dst_ref=stats.at[d],
            send_sem=stat_send.at[d],
            recv_sem=stat_recv.at[d],
            device_id=peer(d),
            device_id_type=MESH,
        )

    for d in range(1, n):
        stat_copy(d).start()
    for f in range(F):
        def start_acc(r, _):
            acc[f, r + 1] = xv[f, r].astype(jnp.float32) + cbias_ref[...]
            return 0

        lax.fori_loop(0, H, start_acc, 0)
    for d in range(1, n):
        stat_copy(d).wait_recv()
    total = stats[0]
    for d in range(1, n):
        total = total + stats[d]
    sums = jnp.concatenate(
        [
            jnp.broadcast_to(jnp.sum(total[0:8], axis=0, keepdims=True), (8, C)),
            jnp.broadcast_to(jnp.sum(total[8:16], axis=0, keepdims=True), (8, C)),
        ],
        axis=0,
    )
    per_group = C // GROUPS
    channel = lax.broadcasted_iota(jnp.int32, (C, C), 0)
    other = lax.broadcasted_iota(jnp.int32, (C, C), 1)
    first = (other // per_group) * per_group
    member = jnp.where((channel >= first) & (channel < first + per_group), 1.0, 0.0)
    cells = 1.0 * F * H * W * per_group * n
    moments = (
        jnp.dot(
            sums,
            member.astype(jnp.float32),
            preferred_element_type=jnp.float32,
            precision=lax.Precision.HIGHEST,
        )
        / cells
    )
    mean = moments[0:1]
    var = jnp.maximum(moments[8:9] - mean * mean, 0.0)
    half_scale = lax.rsqrt(var + epsilon) * gain_ref[...] * 0.5
    half_bias = nbias_ref[...] * 0.5

    column = lax.broadcasted_iota(jnp.int32, (W, C), 0)

    def activate(raw, put):
        h = (raw.astype(jnp.float32) - mean) * half_scale + half_bias
        a = h + h * jnp.tanh(h)
        put(0, jnp.where(column == 0, 0.0, pltpu.roll(a, 1, 0)).astype(jnp.bfloat16))
        put(1, a.astype(jnp.bfloat16))
        put(2, jnp.where(column == W - 1, 0.0, pltpu.roll(a, W - 1, 0)).astype(jnp.bfloat16))

    for f in range(F):
        def own_row(r, _):
            def put(k, v):
                own3[f, r, :, k * C : (k + 1) * C] = v

            activate(xv[f, r], put)
            return 0

        lax.fori_loop(0, H, own_row, 0)

    @pl.when(has_prev)
    def _():
        for i in range(2):
            halo_copy(i, 0 if i == 0 else H - 1).wait_recv()
        for side in range(2):
            @pl.when(sends_edge[side])
            def _():
                halo_edge(side).start()

    for c in w_copies:
        c.wait()

    def product(lhs, kt, lo=0, hi=3):
        return jnp.dot(
            lhs, wv[kt, :, lo * C : hi * C], preferred_element_type=jnp.float32
        )

    def own_rows(g, _):
        r0 = g * OWN_ROWS
        for kt in range(3):
            count = F - 2 + kt
            if count <= 0:
                continue
            lhs = own3[0:count, pl.ds(r0, OWN_ROWS)].reshape(count * OWN_ROWS * W, C3)
            y = product(lhs, kt)
            for kh in range(3):
                part = y[:, kh * C : (kh + 1) * C].reshape(count, OWN_ROWS, W, C)
                acc[2 - kt : 2 - kt + count, pl.ds(r0 + 2 - kh, OWN_ROWS)] += part
        return 0

    lax.fori_loop(0, H // OWN_ROWS, own_rows, 0)

    for side in range(2):
        kh = 0 if side == 0 else 2
        at = 1 if side == 0 else H

        @pl.when(gets_edge[side])
        def _():
            own_edge(side).wait_recv()
            for f in range(F):
                def put(k, v):
                    edge3[f, :, k * C : (k + 1) * C] = v

                activate(eown[side, f, 0], put)
            for kt in range(3):
                count = F - 2 + kt
                if count > 0:
                    lhs = edge3[0:count].reshape(count * W, C3)
                    acc[2 - kt : 2 - kt + count, at] += product(lhs, kt, kh, kh + 1).reshape(
                        count, W, C
                    )

    @pl.when(has_prev)
    def _():
        def halo_row(i, _):
            r = row_of(i)

            @pl.when(i >= 2)
            def _():
                halo_copy(i, r).wait_recv()

            for f in range(2):
                def put(k, v):
                    halo3[f, :, k * C : (k + 1) * C] = v

                activate(hraw[f, r], put)
            y = product(halo3[...].reshape(2 * W, C3), 0)
            z = product(halo3[1], 1)
            for kh in range(3):
                cols = slice(kh * C, (kh + 1) * C)
                acc[0, r + 2 - kh] += y[:W, cols] + z[:, cols]
                acc[1, r + 2 - kh] += y[W:, cols]
            return 0

        lax.fori_loop(0, 2, halo_row, 0)
        for side in range(2):
            kh = 0 if side == 0 else 2
            at = 1 if side == 0 else H

            @pl.when(gets_edge[side])
            def _():
                halo_edge(side).wait_recv()
                for f in range(2):
                    def put(k, v):
                        halo3[f, :, k * C : (k + 1) * C] = v

                    activate(ehalo[side, f, 0], put)
                y = product(halo3[...].reshape(2 * W, C3), 0, kh, kh + 1)
                z = product(halo3[1], 1, kh, kh + 1)
                acc[0, at] += y[:W] + z
                acc[1, at] += y[W:]

        lax.fori_loop(2, H, halo_row, 0)

    for f in range(F):
        def finish(r, _):
            out_ref[f, r] = acc[f, r + 1].astype(out_ref.dtype)
            return 0

        lax.fori_loop(0, H, finish, 0)

    for d in range(1, n):
        stat_copy(d).wait_send()

    @pl.when(has_next)
    def _():
        for i in range(H):
            halo_copy(i, 0 if i == 0 else H - 1 if i == 1 else i - 1).wait_send()

    for side in range(2):
        @pl.when(sends_edge[side])
        def _():
            own_edge(side).wait_send()

            @pl.when(has_prev)
            def _():
                halo_edge(side).wait_send()


def shards(T, R, inputs, norm_gain, norm_bias, conv_weight, conv_bias):
    _, F, H, W, C = inputs.shape
    n = T * R
    vmem = pl.BlockSpec(memory_space=pltpu.VMEM)
    anywhere = pl.BlockSpec(memory_space=pl.ANY)
    dma = pltpu.SemaphoreType.DMA
    out = pl.pallas_call(
        functools.partial(block_kernel, T, R),
        out_shape=jax.ShapeDtypeStruct((F, H, W, C), inputs.dtype),
        in_specs=[anywhere, vmem, vmem, anywhere, vmem],
        out_specs=vmem,
        scratch_shapes=[
            pltpu.VMEM((F, H, W, C), jnp.bfloat16),
            pltpu.VMEM((3, 3 * C, 3 * C), jnp.bfloat16),
            pltpu.VMEM((2, H, W, C), jnp.bfloat16),
            pltpu.VMEM((2, F, 1, W, C), jnp.bfloat16),
            pltpu.VMEM((2, 2, 1, W, C), jnp.bfloat16),
            pltpu.VMEM((F, H, W, 3 * C), jnp.bfloat16),
            pltpu.VMEM((2, W, 3 * C), jnp.bfloat16),
            pltpu.VMEM((F, W, 3 * C), jnp.bfloat16),
            pltpu.VMEM((F, H + 2, W, C), jnp.float32),
            pltpu.VMEM((n, 16, C), jnp.float32),
            dma((F,)),
            dma((9,)),
            dma((H,)),
            dma((H,)),
            dma((2,)),
            dma((2,)),
            dma((2,)),
            dma((2,)),
            dma((n,)),
            dma((n,)),
        ],
        compiler_params=pltpu.CompilerParams(
            collective_id=0, has_side_effects=True, vmem_limit_bytes=50 * 1024 * 1024
        ),
        name="norm_conv_block",
    )(
        inputs.reshape(F, H, W, C),
        norm_gain.reshape(1, C),
        norm_bias.reshape(1, C),
        conv_weight.reshape(3, 3, 3 * C, C),
        conv_bias.reshape(1, C),
    )
    return out.reshape(inputs.shape)


def solution(mesh):
    placed = (P("batch", "tm", "rows", None, None), P(), P(), P(), P())
    return jax.shard_map(
        functools.partial(shards, mesh.shape["tm"], mesh.shape["rows"]),
        mesh=mesh,
        in_specs=placed,
        out_specs=P("batch", "tm", "rows", None, None),
        check_vma=False,
    )
```

time: 139 us -> 70.9 us (0.51)
  Pallas kernels: 0 us -> 65.5 us
  matrix products: 43.9 us -> 0 us
  waiting for transfers between devices: 36.2 us -> 0 us
  local copies, waits for them, and re-layouts: 23.1 us -> 4.6 us
  other arithmetic: 17 us -> 0 us
  blocking collectives: 12.7 us -> 0 us
  starting transfers between devices: 4.71 us -> 0 us
    pallas_call x0 -> x1, Pallas kernels: none -> 65.5 us  [shards(): pl.pallas_call(functools.partial(block_kernel, T, R), out_shape=jax.Shape...]
    dot_general x9 -> x0, matrix products: 43.9 us -> none  [convolve(): jnp.dot(columns.reshape(-1, 3 * channels), kernel, preferred_element_type...]
    ppermute x3 -> x0, waiting for transfers between devices: 36.2 us -> none  [the longest x1 36.2 us: from_behind(): lax.ppermute(value, axis, [(source, source + steps) for source in range(i...]
    slice x3 -> x0, local copies, waits for them, and re-layouts: 17.1 us -> none  [the longest x1 10.3 us: convolve(): slab_rows[:, :, :, 0:width_dev]]
    psum x1 -> x0, blocking collectives: 12.7 us -> none  [shards(): lax.psum((grouped(chan_sum, per_group), grouped(chan_raw, per_group)), ('...]
    concatenate x9 -> x0, other arithmetic: 10.5 us -> none  [the longest x7 7.53 us: convolve(): jnp.concatenate([slab_rows[:, :, :, 0:width_dev], slab_rows[:, :, :, 1:wi...]
    ppermute x3 -> x0, starting transfers between devices: 4.71 us -> none  [the longest x1 1.92 us: from_behind(): lax.ppermute(value, axis, [(source, source + steps) for source in range(i...]
    convert_element_type x2 -> x0, other arithmetic: 4.26 us -> none  [the longest x1 2.53 us: shards(): active = (normed * jax.nn.sigmoid(normed)).astype(jnp.bfloat16)]
  transfers between devices with their start and end apart: 3 -> 0, of which waited for: 1 -> 0; matrix products, arithmetic and copies ran while one was open for 4% -> 0% of each run, Pallas kernels for 0% -> 0%
where the time goes in v1:
time: 70.9 us; the launch traced here: 70.1 us
  Pallas kernels  65.5 us (92%)
  local copies, waits for them, and re-layouts  4.6 us (6%)
    pallas_call x1, Pallas kernels, shards(): pl.pallas_call(functools.partial(block_kernel, T, R), out_shape=jax.Shape...  65.5 us
    unnamed x3, local copies, waits for them, and re-layouts  2.55 us

profile of v1, /device:TPU:20, one launch (start us, length us, event | category | flops | bytes accessed | tf_op | source)
XLA Modules:
  0.0 70.1 jit_solution(761762361865944843)
XLA Ops:
  0.0 0.7 reshape.19.gain_ref
  0.7 0.7 reshape.20.nbias_ref
  1.4 0.7 reshape.22.cbias_ref
  2.0 0.0 copy-start
  2.1 1.4 %copy-done = bf16[1,2,8,128,384]{4,3,2,1,0:T(8,128)(2,1)S(1)} copy-done((bf16[1,2,8,128,384]{4,3,2,1,0:T(8,128)(2,1)S(1)}, bf16[1,2,8,128,384]{4,3,2,1,0:T(8,128)(2,1)}, u32[]{:S(2)}) %copy-start) | copy-done | bytes 1572888
  3.5 65.5 %norm_conv_block.1 = bf16[2,8,128,384]{3,2,1,0:T(8,128)(2,1)S(1)} custom-call(bf16[2,8,128,384]{3,2,1,0:T(8,128)(2,1)S(1)} %bitcast.4, f32[1,384]{1,0:T(1,128)S(1)} %reshape.19.gain_ref, f32[1,384]{1,0:T(1,128)S(1)} %reshape.20.nbias_ref, bf16[3,3,1152,384]{3,2,1,0:T(8,128)(2,1)} %bitcast.5, f32[1,384]{1,0:T(1,128)S(1)} %reshape.22.cbias_ref), custom_call_target="tpu_custom_call" | custom-call | tf_op jit(solution)/shard_map/norm_conv_block/pallas_call | solution.py:310
  69.0 1.1 %copy.7 = bf16[1,2,8,128,384]{4,3,2,1,0:T(8,128)(2,1)} copy(bf16[1,2,8,128,384]{4,3,2,1,0:T(8,128)(2,1)S(1)} %bitcast.3) | data formatting | bytes 3145728
Async XLA Ops:
  2.0 1.4 %copy-start = (bf16[1,2,8,128,384]{4,3,2,1,0:T(8,128)(2,1)S(1)}, bf16[1,2,8,128,384]{4,3,2,1,0:T(8,128)(2,1)}, u32[]{:S(2)}) copy-start(bf16[1,2,8,128,384]{4,3,2,1,0:T(8,128)(2,1)} %param.5) | copy-start | bytes 4718596

commit v2 on v1

--- a/solution.py
+++ b/solution.py
@@ -10,13 +10,14 @@
 GROUPS = 32
 MESH = pl.DeviceIdType.MESH
 OWN_ROWS = 2
+EARLY = 1
 
 epsilon = 1e-06
 
 
 def block_kernel(
-    T, R, x_hbm, gain_ref, nbias_ref, w_hbm, cbias_ref, out_ref,
-    xv, wv, hraw, eown, ehalo, own3, halo3, edge3, acc, stats,
+    T, R, x_hbm, gain_hbm, nbias_hbm, w_hbm, cbias_hbm, out_ref,
+    params, p_sem, xv, wv, hraw, eown, ehalo, own3, halo3, edge3, acc, stats,
     x_sem, w_sem, halo_send, halo_recv, eown_send, eown_recv,
     ehalo_send, ehalo_recv, stat_send, stat_recv,
 ):
@@ -39,10 +40,14 @@
         for kt in range(3)
         for kh in range(3)
     ]
+    p_copies = [
+        pltpu.make_async_copy(p, params.at[k, 0], p_sem.at[k])
+        for k, p in enumerate((gain_hbm, nbias_hbm, cbias_hbm))
+    ]
     barrier = pltpu.get_barrier_semaphore()
     for d in range(1, n):
         pl.semaphore_signal(barrier, inc=1, device_id=peer(d), device_id_type=MESH)
-    for c in x_copies:
+    for c in x_copies + p_copies:
         c.start()
     pl.semaphore_wait(barrier, n - 1)
 
@@ -89,7 +94,7 @@
 
     @pl.when(has_next)
     def _():
-        for i in range(H):
+        for i in range(EARLY):
             halo_copy(i, 0 if i == 0 else H - 1 if i == 1 else i - 1).start()
 
     for side in range(2):
@@ -125,9 +130,17 @@
 
     for d in range(1, n):
         stat_copy(d).start()
+
+    @pl.when(has_next)
+    def _():
+        for i in range(EARLY, H):
+            halo_copy(i, 0 if i == 0 else H - 1 if i == 1 else i - 1).start()
+
+    for c in p_copies:
+        c.wait()
     for f in range(F):
         def start_acc(r, _):
-            acc[f, r + 1] = xv[f, r].astype(jnp.float32) + cbias_ref[...]
+            acc[f, r + 1] = xv[f, r].astype(jnp.float32) + params[2]
             return 0
 
         lax.fori_loop(0, H, start_acc, 0)
@@ -160,8 +173,8 @@
     )
     mean = moments[0:1]
     var = jnp.maximum(moments[8:9] - mean * mean, 0.0)
-    half_scale = lax.rsqrt(var + epsilon) * gain_ref[...] * 0.5
-    half_bias = nbias_ref[...] * 0.5
+    half_scale = lax.rsqrt(var + epsilon) * params[0] * 0.5
+    half_bias = params[1] * 0.5
 
     column = lax.broadcasted_iota(jnp.int32, (W, C), 0)
 
@@ -198,6 +211,11 @@
         return jnp.dot(
             lhs, wv[kt, :, lo * C : hi * C], preferred_element_type=jnp.float32
         )
+
+    def finish(r, _):
+        for f in range(F):
+            out_ref[f, r] = acc[f, r + 1].astype(out_ref.dtype)
+        return 0
 
     def own_rows(g, _):
         r0 = g * OWN_ROWS
@@ -254,6 +272,11 @@
                 cols = slice(kh * C, (kh + 1) * C)
                 acc[0, r + 2 - kh] += y[:W, cols] + z[:, cols]
                 acc[1, r + 2 - kh] += y[W:, cols]
+
+            @pl.when(i >= 2)
+            def _():
+                finish(i - 2, 0)
+
             return 0
 
         lax.fori_loop(0, 2, halo_row, 0)
@@ -275,12 +298,10 @@
                 acc[1, at] += y[W:]
 
         lax.fori_loop(2, H, halo_row, 0)
-
-    for f in range(F):
-        def finish(r, _):
-            out_ref[f, r] = acc[f, r + 1].astype(out_ref.dtype)
-            return 0
-
+        lax.fori_loop(max(H - 2, 0), H, finish, 0)
+
+    @pl.when(jnp.logical_not(has_prev))
+    def _():
         lax.fori_loop(0, H, finish, 0)
 
     for d in range(1, n):
@@ -305,14 +326,17 @@
     _, F, H, W, C = inputs.shape
     n = T * R
     vmem = pl.BlockSpec(memory_space=pltpu.VMEM)
+    hbm = pl.BlockSpec(memory_space=pltpu.HBM)
     anywhere = pl.BlockSpec(memory_space=pl.ANY)
     dma = pltpu.SemaphoreType.DMA
     out = pl.pallas_call(
         functools.partial(block_kernel, T, R),
         out_shape=jax.ShapeDtypeStruct((F, H, W, C), inputs.dtype),
-        in_specs=[anywhere, vmem, vmem, anywhere, vmem],
+        in_specs=[hbm, anywhere, anywhere, hbm, anywhere],
         out_specs=vmem,
         scratch_shapes=[
+            pltpu.VMEM((3, 1, C), jnp.float32),
+            dma((3,)),
             pltpu.VMEM((F, H, W, C), jnp.bfloat16),
             pltpu.VMEM((3, 3 * C, 3 * C), jnp.bfloat16),
             pltpu.VMEM((2, H, W, C), jnp.bfloat16),
@@ -340,10 +364,10 @@
         name="norm_conv_block",
     )(
         inputs.reshape(F, H, W, C),
-        norm_gain.reshape(1, C),
-        norm_bias.reshape(1, C),
+        norm_gain,
+        norm_bias,
         conv_weight.reshape(3, 3, 3 * C, C),
-        conv_bias.reshape(1, C),
+        conv_bias,
     )
     return out.reshape(inputs.shape)
 

time: 70.9 us -> 46.7 us (0.66)
  Pallas kernels: 65.5 us -> 41.8 us
    pallas_call x1, Pallas kernels: 65.5 us -> 41.8 us  [shards(): pl.pallas_call(functools.partial(block_kernel, T, R), out_shape=jax.Shape...]
    reshape x3 -> x0, local copies, waits for them, and re-layouts: 2.05 us -> none  [the longest x1 0.68 us: shards(): norm_gain.reshape(1, C)]
    unnamed x3 -> x9, local copies, waits for them, and re-layouts: 2.55 us -> 4.6 us
where the time goes in v2:
time: 46.7 us; the launch traced here: 46.4 us
  Pallas kernels  41.8 us (90%)
  local copies, waits for them, and re-layouts  4.6 us (10%)
    pallas_call x1, Pallas kernels, shards(): pl.pallas_call(functools.partial(block_kernel, T, R), out_shape=jax.Shape...  41.8 us
    unnamed x9, local copies, waits for them, and re-layouts  4.6 us

profile of v2, /device:TPU:20, one launch (start us, length us, event | category | flops | bytes accessed | tf_op | source)
XLA Modules:
  0.0 46.4 jit_solution(16594021242193130295)
XLA Ops:
  0.0 0.0 copy-start
  0.0 1.4 %copy-done = bf16[1,2,8,128,384]{4,3,2,1,0:T(8,128)(2,1)S(1)} copy-done((bf16[1,2,8,128,384]{4,3,2,1,0:T(8,128)(2,1)S(1)}, bf16[1,2,8,128,384]{4,3,2,1,0:T(8,128)(2,1)}, u32[]{:S(2)}) %copy-start) | copy-done | bytes 1572888
  1.4 0.0 copy-start.1
  1.4 0.7 %copy-done.1 = f32[384]{0:T(512)S(1)} copy-done((f32[384]{0:T(512)S(1)}, f32[384]{0:T(512)}, u32[]{:S(2)}) %copy-start.1) | copy-done | bytes 1560
  2.1 0.0 copy-start.2
  2.1 0.7 %copy-done.2 = f32[384]{0:T(512)S(1)} copy-done((f32[384]{0:T(512)S(1)}, f32[384]{0:T(512)}, u32[]{:S(2)}) %copy-start.2) | copy-done | bytes 1560
  2.8 0.0 copy-start.3
  2.8 0.7 %copy-done.3 = f32[384]{0:T(512)S(1)} copy-done((f32[384]{0:T(512)S(1)}, f32[384]{0:T(512)}, u32[]{:S(2)}) %copy-start.3) | copy-done | bytes 1560
  3.5 41.8 %norm_conv_block.1 = bf16[2,8,128,384]{3,2,1,0:T(8,128)(2,1)S(1)} custom-call(bf16[2,8,128,384]{3,2,1,0:T(8,128)(2,1)S(1)} %bitcast.4, f32[384]{0:T(512)S(1)} %copy-done.1, f32[384]{0:T(512)S(1)} %copy-done.2, bf16[3,3,1152,384]{3,2,1,0:T(8,128)(2,1)} %bitcast.5, f32[384]{0:T(512)S(1)} %copy-done.3), custom_call_target="tpu_custom_call" | custom-call | tf_op jit(solution)/shard_map/norm_conv_block/pallas_call | solution.py:332
  45.3 1.1 %copy.7 = bf16[1,2,8,128,384]{4,3,2,1,0:T(8,128)(2,1)} copy(bf16[1,2,8,128,384]{4,3,2,1,0:T(8,128)(2,1)S(1)} %bitcast.3) | data formatting | bytes 3145728
Async XLA Ops:
  0.0 1.4 %copy-start = (bf16[1,2,8,128,384]{4,3,2,1,0:T(8,128)(2,1)S(1)}, bf16[1,2,8,128,384]{4,3,2,1,0:T(8,128)(2,1)}, u32[]{:S(2)}) copy-start(bf16[1,2,8,128,384]{4,3,2,1,0:T(8,128)(2,1)} %param.5) | copy-start | bytes 4718596
  1.4 0.7 %copy-start.1 = (f32[384]{0:T(512)S(1)}, f32[384]{0:T(512)}, u32[]{:S(2)}) copy-start(f32[384]{0:T(512)} %gain_hbm.1) | copy-start | bytes 4612
  2.1 0.7 %copy-start.2 = (f32[384]{0:T(512)S(1)}, f32[384]{0:T(512)}, u32[]{:S(2)}) copy-start(f32[384]{0:T(512)} %nbias_hbm.1) | copy-start | bytes 4612
  2.8 0.7 %copy-start.3 = (f32[384]{0:T(512)S(1)}, f32[384]{0:T(512)}, u32[]{:S(2)}) copy-start(f32[384]{0:T(512)} %cbias_hbm.1) | copy-start | bytes 4612

commit v3 on v2

--- a/solution.py
+++ b/solution.py
@@ -325,6 +325,10 @@
 def shards(T, R, inputs, norm_gain, norm_bias, conv_weight, conv_bias):
     _, F, H, W, C = inputs.shape
     n = T * R
+
+    def pin(a):
+        return pltpu.with_memory_space_constraint(a, pltpu.HBM)
+
     vmem = pl.BlockSpec(memory_space=pltpu.VMEM)
     hbm = pl.BlockSpec(memory_space=pltpu.HBM)
     anywhere = pl.BlockSpec(memory_space=pl.ANY)
@@ -363,11 +367,11 @@
         ),
         name="norm_conv_block",
     )(
-        inputs.reshape(F, H, W, C),
-        norm_gain,
-        norm_bias,
-        conv_weight.reshape(3, 3, 3 * C, C),
-        conv_bias,
+        pin(inputs.reshape(F, H, W, C)),
+        pin(norm_gain),
+        pin(norm_bias),
+        pin(conv_weight.reshape(3, 3, 3 * C, C)),
+        pin(conv_bias),
     )
     return out.reshape(inputs.shape)
 

time: 46.7 us -> 43.3 us (0.927)
  local copies, waits for them, and re-layouts: 4.6 us -> 1.15 us
    unnamed x9 -> x1, local copies, waits for them, and re-layouts: 4.6 us -> 1.15 us
where the time goes in v3:
time: 43.3 us; the launch traced here: 43.2 us
  Pallas kernels  42 us (97%)
  local copies, waits for them, and re-layouts  1.15 us (3%)
    pallas_call x1, Pallas kernels, shards(): pl.pallas_call(functools.partial(block_kernel, T, R), out_shape=jax.Shape...  42 us
    unnamed x1, local copies, waits for them, and re-layouts  1.15 us

profile of v3, /device:TPU:20, one launch (start us, length us, event | category | flops | bytes accessed | tf_op | source)
XLA Modules:
  0.0 43.2 jit_solution(7254307973367055148)
XLA Ops:
  0.0 42.0 %norm_conv_block.1 = bf16[2,8,128,384]{3,2,1,0:T(8,128)(2,1)S(1)} custom-call(bf16[2,8,128,384]{3,2,1,0:T(8,128)(2,1)} %bitcast.5, f32[384]{0:T(512)} %gain_hbm.1, f32[384]{0:T(512)} %nbias_hbm.1, bf16[3,3,1152,384]{3,2,1,0:T(8,128)(2,1)} %bitcast.4, f32[384]{0:T(512)} %cbias_hbm.1), custom_call_target="tpu_custom_call" | custom-call | tf_op jit(solution)/shard_map/norm_conv_block/pallas_call | solution.py:336
  42.1 1.1 %copy.7 = bf16[1,2,8,128,384]{4,3,2,1,0:T(8,128)(2,1)} copy(bf16[1,2,8,128,384]{4,3,2,1,0:T(8,128)(2,1)S(1)} %bitcast.3) | data formatting | bytes 3145728

commit v4 on v3

--- a/solution.py
+++ b/solution.py
@@ -9,8 +9,8 @@
 
 GROUPS = 32
 MESH = pl.DeviceIdType.MESH
-OWN_ROWS = 2
-EARLY = 1
+OWN_ROWS = 4
+EARLY = 2
 
 epsilon = 1e-06
 

time: 43.3 us -> 43.3 us (level)
  no operation moved by 1% of the time
where the time goes in v4:
time: 43.3 us; the launch traced here: 43.2 us
  Pallas kernels  42 us (97%)
  local copies, waits for them, and re-layouts  1.15 us (3%)
    pallas_call x1, Pallas kernels, shards(): pl.pallas_call(functools.partial(block_kernel, T, R), out_shape=jax.Shape...  42 us
    unnamed x1, local copies, waits for them, and re-layouts  1.15 us

profile of v4, /device:TPU:20, one launch (start us, length us, event | category | flops | bytes accessed | tf_op | source)
XLA Modules:
  0.0 43.2 jit_solution(18122671532430666689)
XLA Ops:
  0.0 42.0 %norm_conv_block.1 = bf16[2,8,128,384]{3,2,1,0:T(8,128)(2,1)S(1)} custom-call(bf16[2,8,128,384]{3,2,1,0:T(8,128)(2,1)} %bitcast.5, f32[384]{0:T(512)} %gain_hbm.1, f32[384]{0:T(512)} %nbias_hbm.1, bf16[3,3,1152,384]{3,2,1,0:T(8,128)(2,1)} %bitcast.4, f32[384]{0:T(512)} %cbias_hbm.1), custom_call_target="tpu_custom_call" | custom-call | tf_op jit(solution)/shard_map/norm_conv_block/pallas_call | solution.py:336
  42.1 1.1 %copy.7 = bf16[1,2,8,128,384]{4,3,2,1,0:T(8,128)(2,1)} copy(bf16[1,2,8,128,384]{4,3,2,1,0:T(8,128)(2,1)S(1)} %bitcast.3) | data formatting | bytes 3145728
